TPU v7x, 32 devices: a whole 2x2x4 slice. The times are simulated.
32 devices in a mesh: gx: 4 (over y, x), gy: 4 (over z), gz: 2 (over core).
Axes of the slice: x: 2, y: 2, z: 4, core: 2. Of those that a mesh axis runs over, the one named last changes fastest.
Arguments:
- residual_in: float32 [2, 4, 64, 64, 256], P(None, None, 'gx', 'gy', 'gz'), may hold values from -15 to 15
- reaction: float32 [4, 64, 64, 256], P(None, 'gx', 'gy', 'gz'), may hold values from 0.5 to 2
- transport: float32 [4, 64, 64, 256], P(None, 'gx', 'gy', 'gz'), may hold values from 0.2 to 1
- congestion: float32 [4, 64, 64, 256], P(None, 'gx', 'gy', 'gz'), may hold values from 0.5 to 1.5
Outputs:
- newton_update: float32 [2, 4, 64, 64, 256], P(None, None, 'gx', 'gy', 'gz')
All inputs are finite; a program needn't handle non-finite values.
Results may differ from a plain program's by a relative error of at most 0.0003.
Values sent between devices are 32-bit elements; how exact they have to be, the bound alone decides.
A program may use at most 128 MiB of HBM per device.

v0:
```python
import jax
import jax.numpy as jnp
from jax import lax
from jax.sharding import PartitionSpec as P

ITERS = 8


time_rate = 1.0


def with_halo(block, sides, width):
    for axis, dim in sides:
        count = lax.axis_size(axis)
        forward = [(i, i + 1) for i in range(count - 1)]
        backward = [(target, source) for source, target in forward]
        low = lax.ppermute(
            lax.slice_in_dim(block, block.shape[dim] - width, None, axis=dim), axis, forward
        )
        high = lax.ppermute(lax.slice_in_dim(block, 0, width, axis=dim), axis, backward)
        block = jnp.concatenate([low, block, high], axis=dim)
    return block


def stencil(padded):
    center = padded[..., 1:-1, 1:-1, 1:-1]
    beside = padded[..., 2:, 1:-1, 1:-1] + padded[..., :-2, 1:-1, 1:-1]
    beside = beside + padded[..., 1:-1, 2:, 1:-1] + padded[..., 1:-1, :-2, 1:-1]
    beside = beside + padded[..., 1:-1, 1:-1, 2:] + padded[..., 1:-1, 1:-1, :-2]
    return 6.0 * center - beside


def jacobian(vector, lapped, reaction, transport, congestion):
    value_part, density_part = (vector[0], vector[1])
    later = jnp.concatenate([value_part[1:], jnp.zeros_like(value_part[:1])], 0)
    earlier = jnp.concatenate([jnp.zeros_like(density_part[:1]), density_part[:-1]], 0)
    first = (
        time_rate * (value_part - later)
        + lapped[0]
        + reaction * value_part
        - congestion * density_part
    )
    second = (
        time_rate * (density_part - earlier)
        + lapped[1]
        + reaction * density_part
        - transport * lapped[0]
    )
    return jnp.stack([first, second], 0)


def precondition(vector, reaction, transport):
    levels = vector.shape[1]
    diag = time_rate + 6.0 + reaction
    value_levels = [None] * levels
    carry = jnp.zeros_like(vector[0, 0])
    for level in range(levels - 1, -1, -1):
        carry = (vector[0, level] + time_rate * carry) / diag[level]
        value_levels[level] = carry
    density_levels = []
    carry = jnp.zeros_like(vector[1, 0])
    for level in range(levels):
        carry = (
            vector[1, level] + time_rate * carry + 6.0 * transport[level] * value_levels[level]
        ) / diag[level]
        density_levels.append(carry)
    return jnp.stack([jnp.stack(value_levels, 0), jnp.stack(density_levels, 0)], 0)


def lapped_field(search):
    padded = with_halo(search, (("gx", 2), ("gy", 3), ("gz", 4)), 1)
    return stencil(padded)


def least_squares(columns, beta, steps):
    rotations = []
    target = [beta] + [jnp.float32(0.0)] * steps
    upper = []
    for column_index in range(steps):
        column = list(columns[column_index])
        for place, (cosine, sine) in enumerate(rotations):
            upper_entry = cosine * column[place] + sine * column[place + 1]
            lower_entry = -sine * column[place] + cosine * column[place + 1]
            column[place], column[place + 1] = (upper_entry, lower_entry)
        radius = jnp.sqrt(column[column_index] ** 2 + column[column_index + 1] ** 2)
        cosine = column[column_index] / radius
        sine = column[column_index + 1] / radius
        column[column_index] = radius
        rotations.append((cosine, sine))
        target[column_index], target[column_index + 1] = (
            cosine * target[column_index],
            -sine * target[column_index],
        )
        upper.append(column[: column_index + 1])
    solved = [None] * steps
    for row_index in range(steps - 1, -1, -1):
        accum = target[row_index]
        for later_index in range(row_index + 1, steps):
            accum = accum - upper[later_index][row_index] * solved[later_index]
        solved[row_index] = accum / upper[row_index][row_index]
    return solved


def body(residual_in, reaction, transport, congestion):
    beta = jnp.sqrt(lax.psum(jnp.sum(residual_in * residual_in), ("gx", "gy", "gz")))
    basis = [residual_in / beta]
    searches = []
    columns = []
    for column_index in range(ITERS):
        search = precondition(basis[column_index], reaction, transport)
        searches.append(search)
        image = jacobian(search, lapped_field(search), reaction, transport, congestion)
        local_dots = jnp.stack([jnp.sum(vector * image) for vector in basis])
        totals, whole_square = lax.psum((local_dots, jnp.sum(image * image)), ("gx", "gy", "gz"))
        coeffs = [totals[place] for place in range(len(basis))]
        for coeff, vector in zip(coeffs, basis):
            image = image - coeff * vector
        height = jnp.sqrt(whole_square - jnp.sum(totals * totals))
        basis.append(image / height)
        columns.append(coeffs + [height])
    solved = least_squares(columns, beta, ITERS)
    update = jnp.zeros_like(residual_in)
    for column_index in range(ITERS):
        update = update + solved[column_index] * searches[column_index]
    return update


def solution(mesh):
    placed = (
        P(None, None, "gx", "gy", "gz"),
        P(None, "gx", "gy", "gz"),
        P(None, "gx", "gy", "gz"),
        P(None, "gx", "gy", "gz"),
    )
    return jax.shard_map(
        body, mesh=mesh, in_specs=placed, out_specs=P(None, None, "gx", "gy", "gz"), check_vma=False
    )
```

profile of v0, /device:TPU:0, one launch (start us, length us, event | category | flops | bytes accessed | tf_op | source)
XLA Modules:
  0.0 913.7 jit_solution(5707754039757316582)
XLA Ops:
  2.2 42.2 %psum.119 = f32[]{:T(128)} all-reduce(f32[]{:T(128)} %multiply_reduce_fusion.44), channel_id=1, replica_groups=mesh['gx'=4,'gy'=4,'gz'=2] {'gx','gy','gz'}, use_global_device_ids=true, to_apply=%region_1.0 | all-reduce | flops 1 | bytes 8 | tf_op jit(solution)/shard_map/psum | solution.py:105
  47.4 4.8 collective-permute-start.1
  88.8 43.2 %all-reduce.23 = (f32[]{:T(128)}, f32[1]{0:T(128)}) all-reduce(f32[]{:T(128)} %get-tuple-element.47, f32[1]{0:T(128)} %bitcast.14), channel_id=1, replica_groups=mesh['gx'=4,'gy'=4,'gz'=2] {'gx','gy','gz'}, use_global_device_ids=true, to_apply=%region_5.0 | all-reduce | flops 2 | bytes 16 | tf_op jit(solution)/shard_map/psum | solution.py:114
  137.1 4.8 collective-permute-start.7
  173.2 6.6 fusion.37
  183.5 43.0 %all-reduce.22 = (f32[]{:T(128)}, f32[2]{0:T(128)S(1)}) all-reduce(f32[]{:T(128)} %get-tuple-element.45, f32[2]{0:T(128)S(1)} %pad_maximum_fusion.264), channel_id=1, replica_groups=mesh['gx'=4,'gy'=4,'gz'=2] {'gx','gy','gz'}, use_global_device_ids=true, to_apply=%region_10.0 | all-reduce | flops 3 | bytes 24 | tf_op jit(solution)/shard_map/psum | solution.py:114
  235.1 4.8 collective-permute-start.13
  271.0 6.7 fusion.31
  284.1 43.4 %all-reduce.21 = (f32[]{:T(128)}, f32[3]{0:T(128)S(1)}) all-reduce(f32[]{:T(128)} %get-tuple-element.42, f32[3]{0:T(128)S(1)} %pad_maximum_fusion.265), channel_id=1, replica_groups=mesh['gx'=4,'gy'=4,'gz'=2] {'gx','gy','gz'}, use_global_device_ids=true, to_apply=%region_17.0 | all-reduce | flops 4 | bytes 32 | tf_op jit(solution)/shard_map/psum | solution.py:114
  336.7 4.8 collective-permute-start.19
  372.6 6.5 fusion.25
  386.6 43.1 %all-reduce.20 = (f32[]{:T(128)}, f32[4]{0:T(128)S(1)}) all-reduce(f32[]{:T(128)} %get-tuple-element.38, f32[4]{0:T(128)S(1)} %pad_maximum_fusion.266), channel_id=1, replica_groups=mesh['gx'=4,'gy'=4,'gz'=2] {'gx','gy','gz'}, use_global_device_ids=true, to_apply=%region_25.0 | all-reduce | flops 5 | bytes 40 | tf_op jit(solution)/shard_map/psum | solution.py:114
  432.3 5.3 subtract_divide_fusion.3
  440.0 4.8 collective-permute-start.25
  476.1 6.8 fusion.19
  491.3 43.0 %all-reduce.19 = (f32[]{:T(128)}, f32[5]{0:T(128)S(1)}) all-reduce(f32[]{:T(128)} %get-tuple-element.32, f32[5]{0:T(128)S(1)} %stack.485), channel_id=1, replica_groups=mesh['gx'=4,'gy'=4,'gz'=2] {'gx','gy','gz'}, use_global_device_ids=true, to_apply=%region_34.0 | all-reduce | flops 6 | bytes 48 | tf_op jit(solution)/shard_map/psum | solution.py:114
  537.0 6.3 subtract_divide_fusion.2
  545.7 4.8 collective-permute-start.31
  581.6 6.7 fusion.13
  597.2 43.2 %all-reduce.18 = (f32[]{:T(128)}, f32[6]{0:T(128)S(1)}) all-reduce(f32[]{:T(128)} %get-tuple-element.27, f32[6]{0:T(128)S(1)} %stack.502), channel_id=1, replica_groups=mesh['gx'=4,'gy'=4,'gz'=2] {'gx','gy','gz'}, use_global_device_ids=true, to_apply=%region_44.0 | all-reduce | flops 7 | bytes 56 | tf_op jit(solution)/shard_map/psum | solution.py:114
  642.9 7.4 subtract_divide_fusion.1
  652.7 4.8 collective-permute-start.37
  688.6 6.4 fusion.7
  700.7 4.6 stack.520
  705.3 42.9 %all-reduce.17 = (f32[]{:T(128)}, f32[7]{0:T(128)S(1)}) all-reduce(f32[]{:T(128)} %get-tuple-element.165, f32[7]{0:T(128)S(1)} %stack.520), channel_id=1, replica_groups=mesh['gx'=4,'gy'=4,'gz'=2] {'gx','gy','gz'}, use_global_device_ids=true, to_apply=%region_55.0 | all-reduce | flops 8 | bytes 64 | tf_op jit(solution)/shard_map/psum | solution.py:114
  750.8 8.5 subtract_divide_fusion
  761.8 4.8 collective-permute-start.43
  770.0 4.8 collective-permute-start.45
  835.0 6.7 fusion.1
  847.5 4.9 stack.539
  852.4 43.1 %all-reduce.16 = (f32[8]{0:T(128)S(1)}, f32[]{:T(128)}) all-reduce(f32[8]{0:T(128)S(1)} %stack.539, f32[]{:T(128)} %get-tuple-element.5), channel_id=1, replica_groups=mesh['gx'=4,'gy'=4,'gz'=2] {'gx','gy','gz'}, use_global_device_ids=true, to_apply=%region_65.0 | all-reduce | flops 9 | bytes 72 | tf_op jit(solution)/shard_map/psum | solution.py:114
  908.3 4.9 multiply_add_fusion
  (656 shorter events, 333.2 us)
Async XLA Ops:
  47.4 6.7 collective-permute-start.1
  55.7 6.5 collective-permute-start.3
  68.0 8.7 collective-permute-start.4
  72.3 7.5 collective-permute-start.5
  137.1 6.7 collective-permute-start.7
  145.3 6.5 collective-permute-start.9
  158.2 8.8 collective-permute-start.10
  162.6 7.5 collective-permute-start.11
  235.1 6.7 collective-permute-start.13
  243.3 6.5 collective-permute-start.15
  256.2 8.6 collective-permute-start.16
  260.6 7.3 collective-permute-start.17
  336.7 6.7 collective-permute-start.19
  344.9 6.5 collective-permute-start.21
  357.9 8.6 collective-permute-start.22
  362.2 7.3 collective-permute-start.23
  440.0 6.7 collective-permute-start.25
  448.2 6.5 collective-permute-start.27
  461.2 8.7 collective-permute-start.28
  465.5 7.5 collective-permute-start.29
  545.7 6.7 collective-permute-start.31
  553.9 6.5 collective-permute-start.33
  566.8 8.6 collective-permute-start.34
  571.2 7.3 collective-permute-start.35
  652.7 6.7 collective-permute-start.37
  660.9 6.5 collective-permute-start.39
  673.9 8.6 collective-permute-start.40
  678.2 7.3 collective-permute-start.41
  761.8 6.7 collective-permute-start.43
  770.0 6.8 collective-permute-start.45
  783.5 45.4 %collective-permute-start.46 = (f32[2,4,18,18,1]{3,2,4,1,0:T(8,128)}, f32[2,4,18,18,1]{3,2,4,1,0:T(8,128)}, u32[]{:S(2)}, u32[]{:S(2)}) collective-permute-start(f32[2,4,18,18,1]{3,2,4,1,0:T(8,128)} %copy.548), channel_id=1, source_target_pairs={{1,0},{3,2},{5,4},{7,6},{9,8},{11,10},{13,12},{15,14},{17,16},{19,... | collective-permute-start | bytes 31112 | tf_op jit(solution)/shard_map/ppermute | solution.py:20
  788.1 43.8 %collective-permute-start.47 = (f32[2,4,18,18,1]{3,2,4,1,0:T(8,128)}, f32[2,4,18,18,1]{3,2,4,1,0:T(8,128)}, u32[]{:S(2)}, u32[]{:S(2)}) collective-permute-start(f32[2,4,18,18,1]{3,2,4,1,0:T(8,128)} %copy.550), channel_id=1, source_target_pairs={{0,1},{2,3},{4,5},{6,7},{8,9},{10,11},{12,13},{14,15},{16,17},{18,... | collective-permute-start | bytes 31112 | tf_op jit(solution)/shard_map/ppermute | solution.py:17
  (216 other events, 1632.5 us)
where the time goes:
time: 926 us; the launch traced here: 914 us
  blocking collectives  387 us (42%)
  local copies, waits for them, and re-layouts  165 us (18%)
  starting transfers between devices  141 us (15%)
  other arithmetic  129 us (14%)
  between operations  61.9 us (7%)
  waiting for transfers between devices  30 us (3%)
    psum x8, blocking collectives, body(): lax.psum((local_dots, jnp.sum(image * image)), ('gx', 'gy', 'gz'))  345 us
    ppermute x24, starting transfers between devices, with_halo(): lax.ppermute(lax.slice_in_dim(block, block.shape[dim] - width, None, axis...  110 us
    sub x8, other arithmetic, stencil(): return 6.0 * center - beside  49.9 us
    slice x16, local copies, waits for them, and re-layouts, with_halo(): lax.slice_in_dim(block, 0, width, axis=dim)  43.3 us
    psum x1, blocking collectives, body(): lax.psum(jnp.sum(residual_in * residual_in), ('gx', 'gy', 'gz'))  42.2 us
    div x7, other arithmetic, body(): basis.append(image / height)  36.2 us
    ppermute x24, starting transfers between devices, with_halo(): lax.ppermute(lax.slice_in_dim(block, 0, width, axis=dim), axis, backward)  30.9 us
    unnamed x416, local copies, waits for them, and re-layouts  26.3 us
  transfers between devices with their start and end apart: 48, of which 32 were waited for; matrix products, arithmetic and copies ran while one was open for 5% of the time, Pallas kernels for 0%

commit v1 on v0

v1 whole, which is shorter than its diff:
```python
import functools

import jax
import jax.numpy as jnp
from jax import lax
from jax.experimental import pallas as pl
from jax.experimental.pallas import tpu as pltpu
from jax.sharding import PartitionSpec as P

ITERS = 8
AXES = ("gx", "gy", "gz")
time_rate = 1.0
SCALE = 2.5
BACK = 1.0
PIVOT = 2.5e-3


def pair_index(row, column):
    return column * (column + 1) // 2 + row


def least_squares(columns, beta, steps):
    zero = jnp.zeros_like(beta)
    rotations = []
    target = [beta] + [zero] * steps
    upper = []
    for column_index in range(steps):
        column = list(columns[column_index])
        for place, (cosine, sine) in enumerate(rotations):
            upper_entry = cosine * column[place] + sine * column[place + 1]
            lower_entry = -sine * column[place] + cosine * column[place + 1]
            column[place], column[place + 1] = (upper_entry, lower_entry)
        radius = jnp.sqrt(column[column_index] ** 2 + column[column_index + 1] ** 2)
        inverse = 1.0 / radius
        cosine = column[column_index] * inverse
        sine = column[column_index + 1] * inverse
        column[column_index] = inverse
        rotations.append((cosine, sine))
        target[column_index], target[column_index + 1] = (
            cosine * target[column_index],
            -sine * target[column_index],
        )
        upper.append(column[: column_index + 1])
    solved = [None] * steps
    for row_index in range(steps - 1, -1, -1):
        accum = target[row_index]
        for later_index in range(steps - 1, row_index, -1):
            accum = accum - upper[later_index][row_index] * solved[later_index]
        solved[row_index] = accum * upper[row_index][row_index]
    return solved


def gram_solve(gram, steps):
    size = steps + 1
    work = {(i, j): gram(i, j) for j in range(size) for i in range(j + 1)}
    factor = {}
    worst = None
    for i in range(size):
        ratio = work[i, i] / gram(i, i)
        worst = ratio if worst is None else jnp.where(ratio > worst, worst, ratio)
        pivot = jnp.sqrt(work[i, i])
        inverse = 1.0 / pivot
        factor[i, i] = pivot
        for j in range(i + 1, size):
            factor[i, j] = work[i, j] * inverse
        for a in range(i + 1, size):
            for b in range(a, size):
                work[a, b] = work[a, b] - factor[i, a] * factor[i, b]
    columns = []
    for k in range(steps):
        column = []
        for i in range(k + 2):
            entry = -factor[i, k + 1] * (1.0 / SCALE)
            if i <= k:
                entry = entry + factor[i, k]
            if k > 0 and i <= k - 1:
                entry = entry - factor[i, k - 1] * (BACK / SCALE)
            column.append(entry)
        columns.append(column)
    return least_squares(columns, factor[0, 0], steps), worst


def kernel(
    levels, sizes, residual, reaction, transport, congestion, out, flag,
    basis, inv, weight, couple, search, xin, yout, yin, zout, zin,
    gram, splat, gsend, gall, insem, ssem, rsem, gssem, grsem,
):
    fields = 2 * levels
    nx, ny, nz = residual.shape[1:]
    total = sizes[0] * sizes[1] * sizes[2]
    index = [lax.axis_index(axis) for axis in AXES]
    me = (index[0] * sizes[1] + index[1]) * sizes[2] + index[2]
    lane = lax.broadcasted_iota(jnp.int32, (ny, nz), 1)
    sub = lax.broadcasted_iota(jnp.int32, (ny, nz), 0)

    loads = [
        pltpu.make_async_copy(src, dst, insem.at[place])
        for place, (src, dst) in enumerate(
            ((residual, basis.at[0]), (reaction, inv), (transport, weight), (congestion, couple))
        )
    ]
    for load in loads:
        load.start()

    for buffer in (xin, yin, zin):
        buffer[...] = jnp.zeros_like(buffer)
    gram[...] = jnp.zeros_like(gram)

    def ident(other):
        return (other // (sizes[1] * sizes[2]), (other // sizes[2]) % sizes[1], other % sizes[2])

    barrier = pltpu.get_barrier_semaphore()

    def greet(step, carry):
        pl.semaphore_signal(
            barrier, inc=1, device_id=ident((me + step) % total),
            device_id_type=pl.DeviceIdType.MESH,
        )
        return carry

    lax.fori_loop(1, total, greet, 0)

    def remote(axis, side, slot):
        if axis == 0:
            src, dst = search.at[slot, :, nx - 1 if side == 0 else 0], xin.at[slot, side]
        elif axis == 1:
            src, dst = yout.at[slot, side], yin.at[slot, side]
        else:
            src, dst = zout.at[slot, side], zin.at[slot, side]
        target = list(index)
        target[axis] = index[axis] + (1 if side == 0 else -1)
        return pltpu.make_async_remote_copy(
            src_ref=src, dst_ref=dst,
            send_sem=ssem.at[axis, side, slot], recv_sem=rsem.at[axis, side, slot],
            device_id=tuple(target), device_id_type=pl.DeviceIdType.MESH,
        )

    def sends(axis, side):
        return index[axis] < sizes[axis] - 1 if side == 0 else index[axis] > 0

    def receives(axis, side):
        return index[axis] > 0 if side == 0 else index[axis] < sizes[axis] - 1

    def start(axis, slot):
        odd = index[axis] % 2 == 1
        up, down = sends(axis, 0), sends(axis, 1)

        @pl.when(jnp.logical_and(odd, up))
        def _():
            remote(axis, 0, slot).start()

        @pl.when(down)
        def _():
            remote(axis, 1, slot).start()

        @pl.when(jnp.logical_and(jnp.logical_not(odd), up))
        def _():
            remote(axis, 0, slot).start()

    def wait_sent(axis, slot):
        for side in range(2):
            @pl.when(sends(axis, side))
            def _():
                remote(axis, side, slot).wait_send()

    def wait_received(axis, slot):
        for side in range(2):
            @pl.when(receives(axis, side))
            def _():
                remote(axis, side, slot).wait_recv()

    def precondition(x, vector):
        value, density = [None] * levels, [None] * levels
        carry = None
        for t in range(levels - 1, -1, -1):
            carry = vector[t] if carry is None else vector[t] + carry
            carry = carry * inv[t, x]
            value[t] = carry
        carry = None
        for t in range(levels):
            push = vector[levels + t] + (6.0 * weight[t, x]) * value[t]
            carry = push if carry is None else push + carry
            carry = carry * inv[t, x]
            density[t] = carry
        return value + density

    def publish(x, vector, slot, packs):
        high, low = packs
        found = precondition(x, vector)
        for f in range(fields):
            item = found[f]
            search[slot, f, x] = item
            yout[slot, 0, f, pl.ds(x, 1), :] = item[ny - 1 : ny, :]
            yout[slot, 1, f, pl.ds(x, 1), :] = item[0:1, :]
            place = x * fields + f
            turned = pltpu.roll(item, place, 1)
            high = jnp.where(lane == (place + nz - 1) % nz, turned, high)
            low = jnp.where(lane == place, turned, low)
        return high, low

    def advance(x, k, slot, xlow, xhigh):
        sums, centers = [], []
        zlow, zhigh = zin[slot, 0], zin[slot, 1]
        for f in range(fields):
            center = search[slot, f, x]
            up = jnp.where(sub == 0, yin[slot, 0, f, pl.ds(x, 1), :], pltpu.roll(center, 1, 0))
            down = jnp.where(
                sub == ny - 1, yin[slot, 1, f, pl.ds(x, 1), :], pltpu.roll(center, ny - 1, 0)
            )
            place = x * fields + f
            edge = jnp.where(lane == (place + nz - 1) % nz, zlow, zhigh)
            edge = pltpu.roll(edge, (nz - place) % nz, 1)
            left = pltpu.roll(jnp.where(lane == nz - 1, edge, center), 1, 1)
            right = pltpu.roll(jnp.where(lane == 0, edge, center), nz - 1, 1)
            sums.append(((xlow(f) + xhigh(f)) + (up + down)) + (left + right))
            centers.append(center)
        result = [None] * fields
        for t in range(levels):
            result[t] = sums[t] + couple[t, x] * centers[levels + t]
            result[levels + t] = sums[levels + t] - weight[t, x] * sums[t]
        for f in range(fields):
            item = SCALE * result[f]
            if k > 0:
                item = item - BACK * basis[k - 1, f, x]
            basis[k + 1, f, x] = item
            result[f] = item
        return result

    def dots(k):
        def step(x, accs):
            accs = list(accs)
            for f in range(fields):
                own = basis[k, f, x]
                for j in range(k + 1):
                    other = own if j == k else basis[j, f, x]
                    accs[j] = accs[j] + own * other
            return tuple(accs)

        zero = jnp.zeros((ny, nz), jnp.float32)
        accs = lax.fori_loop(0, nx, step, (zero,) * (k + 1))
        for j in range(k + 1):
            row = pair_index(j, k)
            gram[row : row + 1, :] = jnp.sum(accs[j], axis=0, keepdims=True)

    for load in loads:
        load.wait()

    def invert(x, carry):
        for t in range(levels):
            inv[t, x] = 1.0 / (time_rate + 6.0 + inv[t, x])
        return carry

    lax.fori_loop(0, nx, invert, 0)
    blank = jnp.zeros((ny, nz), jnp.float32)

    def first(x, packs):
        return publish(x, [basis[0, f, x] for f in range(fields)], 0, packs)

    packs = lax.fori_loop(0, nx, first, (blank, blank))
    zout[0, 0], zout[0, 1] = packs
    pl.semaphore_wait(barrier, total - 1)
    start(0, 0)
    start(1, 0)
    start(2, 0)

    for k in range(ITERS):
        slot, later = k % 2, (k + 1) % 2
        last = k == ITERS - 1
        dots(k)
        if k > 0:
            for axis in range(3):
                wait_sent(axis, later)
        wait_received(2, slot)
        wait_received(1, slot)

        def inner(x, packs):
            vector = advance(
                x, k, slot, lambda f: search[slot, f, x - 1], lambda f: search[slot, f, x + 1]
            )
            return packs if last else publish(x, vector, later, packs)

        packs = lax.fori_loop(1, nx - 1, inner, (blank, blank))
        wait_received(0, slot)
        bottom = advance(0, k, slot, lambda f: xin[slot, 0, f], lambda f: search[slot, f, 1])
        if not last:
            packs = publish(0, bottom, later, packs)
        top = advance(
            nx - 1, k, slot, lambda f: search[slot, f, nx - 2], lambda f: xin[slot, 1, f]
        )
        if not last:
            packs = publish(nx - 1, top, later, packs)
            zout[later, 0], zout[later, 1] = packs
            for axis in range(3):
                start(axis, later)

    dots(ITERS)
    for axis in range(3):
        wait_sent(axis, (ITERS - 1) % 2)

    local = jnp.sum(gram[...].T, axis=0, keepdims=True)
    gsend[...] = local
    gall[me] = local

    def spread(step, carry):
        pltpu.make_async_remote_copy(
            src_ref=gsend, dst_ref=gall.at[me], send_sem=gssem, recv_sem=grsem,
            device_id=ident((me + step) % total), device_id_type=pl.DeviceIdType.MESH,
        ).start()
        return carry

    lax.fori_loop(1, total, spread, 0)
    others = gall.at[pl.ds(0, total - 1)]
    pltpu.make_async_copy(others, others, grsem).wait()
    pltpu.make_async_copy(others, others, gssem).wait()
    whole = jnp.sum(gall[...], axis=0)
    splat[...] = jnp.broadcast_to(whole, splat.shape).T

    def entry(i, j):
        row = pair_index(i, j)
        return splat[row : row + 1, :]

    solved, worst = gram_solve(entry, ITERS)
    flag[...] = jnp.broadcast_to(worst, flag.shape)

    def combine(x, carry):
        vector = []
        for f in range(fields):
            item = solved[0] * basis[0, f, x]
            for k in range(1, ITERS):
                item = item + solved[k] * basis[k, f, x]
            vector.append(item)
        found = precondition(x, vector)
        for f in range(fields):
            out[f, x] = found[f]
        return carry

    lax.fori_loop(0, nx, combine, 0)


def fused(sizes, residual, reaction, transport, congestion):
    levels, nx, ny, nz = reaction.shape
    fields = 2 * levels
    total = sizes[0] * sizes[1] * sizes[2]
    pairs = pair_index(ITERS, ITERS) + 1
    assert fields * nx <= nz and pairs <= nz
    f32 = jnp.float32
    hbm = pl.BlockSpec(memory_space=pl.ANY)
    vmem = pl.BlockSpec(memory_space=pltpu.VMEM)
    out, flag = pl.pallas_call(
        functools.partial(kernel, levels, sizes),
        out_shape=(
            jax.ShapeDtypeStruct((fields, nx, ny, nz), f32),
            jax.ShapeDtypeStruct((8, nz), f32),
        ),
        in_specs=[hbm] * 4,
        out_specs=(vmem, vmem),
        scratch_shapes=[
            pltpu.VMEM((ITERS + 1, fields, nx, ny, nz), f32),
            pltpu.VMEM((levels, nx, ny, nz), f32),
            pltpu.VMEM((levels, nx, ny, nz), f32),
            pltpu.VMEM((levels, nx, ny, nz), f32),
            pltpu.VMEM((2, fields, nx, ny, nz), f32),
            pltpu.VMEM((2, 2, fields, ny, nz), f32),
            pltpu.VMEM((2, 2, fields, nx, nz), f32),
            pltpu.VMEM((2, 2, fields, nx, nz), f32),
            pltpu.VMEM((2, 2, ny, nz), f32),
            pltpu.VMEM((2, 2, ny, nz), f32),
            pltpu.VMEM((nz, nz), f32),
            pltpu.VMEM((nz, nz), f32),
            pltpu.VMEM((1, nz), f32),
            pltpu.VMEM((total, 1, nz), f32),
            pltpu.SemaphoreType.DMA((4,)),
            pltpu.SemaphoreType.DMA((3, 2, 2)),
            pltpu.SemaphoreType.DMA((3, 2, 2)),
            pltpu.SemaphoreType.DMA,
            pltpu.SemaphoreType.DMA,
        ],
        compiler_params=pltpu.CompilerParams(
            collective_id=0, has_side_effects=True, vmem_limit_bytes=40 * 1024 * 1024
        ),
        name="krylov",
    )(residual.reshape((fields, nx, ny, nz)), reaction, transport, congestion)
    return out.reshape(residual.shape), flag


def neighbours(field):
    total = 0.0
    for axis, dim in (("gx", 2), ("gy", 3), ("gz", 4)):
        count = lax.axis_size(axis)
        size = field.shape[dim]
        forward = [(i, i + 1) for i in range(count - 1)]
        backward = [(target, source) for source, target in forward]
        low = lax.ppermute(lax.slice_in_dim(field, size - 1, size, axis=dim), axis, forward)
        high = lax.ppermute(lax.slice_in_dim(field, 0, 1, axis=dim), axis, backward)
        below = jnp.concatenate([low, lax.slice_in_dim(field, 0, size - 1, axis=dim)], dim)
        above = jnp.concatenate([lax.slice_in_dim(field, 1, size, axis=dim), high], dim)
        total = total + below + above
    return total


def jacobian(vector, reaction, transport, congestion):
    lapped = 6.0 * vector - neighbours(vector)
    value_part, density_part = (vector[0], vector[1])
    later = jnp.concatenate([value_part[1:], jnp.zeros_like(value_part[:1])], 0)
    earlier = jnp.concatenate([jnp.zeros_like(density_part[:1]), density_part[:-1]], 0)
    first = (
        time_rate * (value_part - later)
        + lapped[0]
        + reaction * value_part
        - congestion * density_part
    )
    second = (
        time_rate * (density_part - earlier)
        + lapped[1]
        + reaction * density_part
        - transport * lapped[0]
    )
    return jnp.stack([first, second], 0)


def precondition(vector, reaction, transport):
    levels = vector.shape[1]
    diag = time_rate + 6.0 + reaction
    value_levels = [None] * levels
    carry = jnp.zeros_like(vector[0, 0])
    for level in range(levels - 1, -1, -1):
        carry = (vector[0, level] + time_rate * carry) / diag[level]
        value_levels[level] = carry
    density_levels = []
    carry = jnp.zeros_like(vector[1, 0])
    for level in range(levels):
        carry = (
            vector[1, level] + time_rate * carry + 6.0 * transport[level] * value_levels[level]
        ) / diag[level]
        density_levels.append(carry)
    return jnp.stack([jnp.stack(value_levels, 0), jnp.stack(density_levels, 0)], 0)


def arnoldi(residual, reaction, transport, congestion):
    dims = tuple(range(1, residual.ndim + 1))
    beta = jnp.sqrt(lax.psum(jnp.sum(residual * residual), AXES))
    basis = jnp.zeros((ITERS + 1,) + residual.shape, residual.dtype).at[0].set(residual / beta)
    heights = jnp.zeros((ITERS, ITERS + 1), residual.dtype)

    def step(c, state):
        basis, heights = state
        search = precondition(basis[c], reaction, transport)
        image = jacobian(search, reaction, transport, congestion)
        coeffs = lax.psum(jnp.sum(basis * image[None], axis=dims), AXES)
        image = image - jnp.sum(coeffs.reshape((-1,) + (1,) * residual.ndim) * basis, axis=0)
        height = jnp.sqrt(lax.psum(jnp.sum(image * image), AXES))
        basis = basis.at[c + 1].set(image / height)
        return basis, heights.at[c].set(coeffs.at[c + 1].set(height))

    basis, heights = lax.fori_loop(0, ITERS, step, (basis, heights))
    columns = [[heights[c, i] for i in range(c + 2)] for c in range(ITERS)]
    solved = least_squares(columns, beta, ITERS)
    mixed = sum(solved[c] * basis[c] for c in range(ITERS))
    return precondition(mixed, reaction, transport)


def body(sizes, residual_in, reaction, transport, congestion):
    update, flag = fused(sizes, residual_in, reaction, transport, congestion)
    return lax.cond(
        flag[0, 0] > PIVOT,
        lambda update, *rest: update,
        lambda update, *rest: arnoldi(*rest),
        update, residual_in, reaction, transport, congestion,
    )


def solution(mesh):
    placed = (
        P(None, None, "gx", "gy", "gz"),
        P(None, "gx", "gy", "gz"),
        P(None, "gx", "gy", "gz"),
        P(None, "gx", "gy", "gz"),
    )
    sizes = tuple(mesh.shape[axis] for axis in AXES)
    return jax.shard_map(
        functools.partial(body, sizes), mesh=mesh, in_specs=placed,
        out_specs=P(None, None, "gx", "gy", "gz"), check_vma=False,
    )
```

time: 926 us -> 75.5 us (0.08); the launches traced: 914 us -> 75.3 us
  blocking collectives: 387 us -> 0 us
  local copies, waits for them, and re-layouts: 165 us -> 2.78 us
  starting transfers between devices: 141 us -> 0 us
  other arithmetic: 129 us -> 0 us
  Pallas kernels: 0 us -> 71.7 us
  between operations: 61.9 us -> 0.67 us
  waiting for transfers between devices: 30 us -> 0 us
    psum x9 -> x0, blocking collectives: 387 us -> none  [the longest x8 345 us: body(): lax.psum((local_dots, jnp.sum(image * image)), ('gx', 'gy', 'gz'))]
    ppermute x48 -> x0, starting transfers between devices: 141 us -> none  [the longest x24 110 us: with_halo(): lax.ppermute(lax.slice_in_dim(block, block.shape[dim] - width, None, axis...]
    slice x31 -> x1, local copies, waits for them, and re-layouts: 72.5 us -> 0.51 us  [body(): flag[0, 0] > PIVOT]
    pallas_call x0 -> x1, Pallas kernels: none -> 71.7 us  [fused(): pl.pallas_call(functools.partial(kernel, levels, sizes), out_shape=(jax.S...]
    ppermute x32 -> x0, local copies, waits for them, and re-layouts: 50.2 us -> none  [the longest x16 25.1 us: with_halo(): lax.ppermute(lax.slice_in_dim(block, 0, width, axis=dim), axis, backward)]
    sub x8 -> x0, other arithmetic: 49.9 us -> none  [stencil(): return 6.0 * center - beside]
    div x16 -> x0, other arithmetic: 37.6 us -> none  [the longest x7 36.2 us: body(): basis.append(image / height)]
    ppermute x48 -> x0, waiting for transfers between devices: 30 us -> none  [the longest x24 24.7 us: with_halo(): lax.ppermute(lax.slice_in_dim(block, block.shape[dim] - width, None, axis...]
  transfers between devices with their start and end apart: 48 -> 0, of which waited for: 32 -> 0; matrix products, arithmetic and copies ran while one was open for 5% -> 0% of each run, Pallas kernels for 0% -> 0%
where the time goes in v1:
time: 75.5 us; the launch traced here: 75.3 us
  Pallas kernels  71.7 us (95%)
  local copies, waits for them, and re-layouts  2.78 us (4%)
    pallas_call x1, Pallas kernels, fused(): pl.pallas_call(functools.partial(kernel, levels, sizes), out_shape=(jax.S...  71.7 us
    unnamed x1, local copies, waits for them, and re-layouts  2.27 us

profile of v1, /device:TPU:0, one launch (start us, length us, event | category | flops | bytes accessed | tf_op | source)
XLA Modules:
  0.0 75.3 jit_solution(5340380272382313085)
XLA Ops:
  0.0 71.7 %krylov.1 = (f32[8,16,16,128]{3,2,1,0:T(8,128)}, f32[8,128]{1,0:T(8,128)S(1)}) custom-call(f32[8,16,16,128]{3,2,1,0:T(8,128)} %bitcast.256, f32[4,16,16,128]{3,2,1,0:T(8,128)} %reaction.1, f32[4,16,16,128]{3,2,1,0:T(8,128)} %transport.1, f32[4,16,16,128]{3,2,1,0:T(8,128)} %congestion.1), custom_call_target="tpu_custom_call" | custom-call | tf_op jit(solution)/shard_map/krylov/pallas_call | solution.py:349
  71.7 0.5 slice.663
  72.8 0.2 conditional.1
  73.1 2.3 %copy.48 = f32[2,4,16,16,128]{4,3,2,1,0:T(8,128)} copy(f32[2,4,16,16,128]{4,3,2,1,0:T(8,128)} %get-tuple-element.260) | data formatting | bytes 2097152

commit v2 on v1

--- a/solution.py
+++ b/solution.py
@@ -13,6 +13,7 @@
 SCALE = 2.5
 BACK = 1.0
 PIVOT = 2.5e-3
+PLANES = 2
 
 
 def pair_index(row, column):
@@ -184,47 +185,64 @@
             density[t] = carry
         return value + density
 
-    def publish(x, vector, slot, packs):
+    def publish(planes, vectors, slot, packs):
         high, low = packs
-        found = precondition(x, vector)
-        for f in range(fields):
-            item = found[f]
-            search[slot, f, x] = item
-            yout[slot, 0, f, pl.ds(x, 1), :] = item[ny - 1 : ny, :]
-            yout[slot, 1, f, pl.ds(x, 1), :] = item[0:1, :]
+        founds = [precondition(x, vector) for x, vector in zip(planes, vectors)]
+        for x, found in zip(planes, founds):
+            for f in range(fields):
+                place = x * fields + f
+                turned = pltpu.roll(found[f], place, 1)
+                high = jnp.where(lane == (place + nz - 1) % nz, turned, high)
+                low = jnp.where(lane == place, turned, low)
+        for x, found in zip(planes, founds):
+            for f in range(fields):
+                search[slot, f, x] = found[f]
+                yout[slot, 0, f, pl.ds(x, 1), :] = found[f][ny - 1 : ny, :]
+                yout[slot, 1, f, pl.ds(x, 1), :] = found[f][0:1, :]
+        return high, low
+
+    def spatial(k, slot, planes):
+        founds = [spatial_plane(k, slot, *plane) for plane in planes]
+        for (x, _, _), found in zip(planes, founds):
+            for f in range(fields):
+                basis[k + 1, f, x] = found[f]
+
+    def spatial_plane(k, slot, x, xlow, xhigh):
+        def around(f):
+            center = search[slot, f, x]
+            up = jnp.where(sub == 0, 0.0, pltpu.roll(center, 1, 0))
+            down = jnp.where(sub == ny - 1, 0.0, pltpu.roll(center, ny - 1, 0))
             place = x * fields + f
-            turned = pltpu.roll(item, place, 1)
-            high = jnp.where(lane == (place + nz - 1) % nz, turned, high)
-            low = jnp.where(lane == place, turned, low)
-        return high, low
-
-    def advance(x, k, slot, xlow, xhigh):
-        sums, centers = [], []
-        zlow, zhigh = zin[slot, 0], zin[slot, 1]
-        for f in range(fields):
-            center = search[slot, f, x]
-            up = jnp.where(sub == 0, yin[slot, 0, f, pl.ds(x, 1), :], pltpu.roll(center, 1, 0))
-            down = jnp.where(
-                sub == ny - 1, yin[slot, 1, f, pl.ds(x, 1), :], pltpu.roll(center, ny - 1, 0)
-            )
-            place = x * fields + f
-            edge = jnp.where(lane == (place + nz - 1) % nz, zlow, zhigh)
+            edge = jnp.where(lane == (place + nz - 1) % nz, zin[slot, 0], zin[slot, 1])
             edge = pltpu.roll(edge, (nz - place) % nz, 1)
             left = pltpu.roll(jnp.where(lane == nz - 1, edge, center), 1, 1)
             right = pltpu.roll(jnp.where(lane == 0, edge, center), nz - 1, 1)
-            sums.append(((xlow(f) + xhigh(f)) + (up + down)) + (left + right))
-            centers.append(center)
-        result = [None] * fields
+            return ((xlow(f) + xhigh(f)) + (up + down)) + (left + right)
+
+        found = [None] * fields
         for t in range(levels):
-            result[t] = sums[t] + couple[t, x] * centers[levels + t]
-            result[levels + t] = sums[levels + t] - weight[t, x] * sums[t]
-        for f in range(fields):
-            item = SCALE * result[f]
-            if k > 0:
-                item = item - BACK * basis[k - 1, f, x]
-            basis[k + 1, f, x] = item
-            result[f] = item
-        return result
+            value = around(t)
+            density = around(levels + t) - weight[t, x] * value
+            value = value + couple[t, x] * search[slot, levels + t, x]
+            for f, item in ((t, value), (levels + t, density)):
+                item = SCALE * item
+                if k > 0:
+                    item = item - BACK * basis[k - 1, f, x]
+                found[f] = item
+        return found
+
+    def finish(x, k, slot):
+        def rows(f):
+            low, high = yin[slot, 0, f, pl.ds(x, 1), :], yin[slot, 1, f, pl.ds(x, 1), :]
+            return SCALE * jnp.where(sub == 0, low, jnp.where(sub == ny - 1, high, 0.0))
+
+        vector = [None] * fields
+        for t in range(levels - 1, -1, -1):
+            value = rows(t)
+            density = rows(levels + t) - weight[t, x] * value
+            for f, item in ((t, value), (levels + t, density)):
+                vector[f] = basis[k + 1, f, x] + item
+        return vector
 
     def dots(k):
         def step(x, accs):
@@ -254,9 +272,11 @@
     blank = jnp.zeros((ny, nz), jnp.float32)
 
     def first(x, packs):
-        return publish(x, [basis[0, f, x] for f in range(fields)], 0, packs)
-
-    packs = lax.fori_loop(0, nx, first, (blank, blank))
+        planes = [x * PLANES + place for place in range(PLANES)]
+        vectors = [[basis[0, f, x] for f in range(fields)] for x in planes]
+        return publish(planes, vectors, 0, packs)
+
+    packs = lax.fori_loop(0, nx // PLANES, first, (blank, blank))
     zout[0, 0], zout[0, 1] = packs
     pl.semaphore_wait(barrier, total - 1)
     start(0, 0)
@@ -271,24 +291,42 @@
             for axis in range(3):
                 wait_sent(axis, later)
         wait_received(2, slot)
+
+        def inner(step, carry):
+            spatial(k, slot, [
+                (
+                    x,
+                    lambda f, x=x: search[slot, f, x - 1],
+                    lambda f, x=x: search[slot, f, x + 1],
+                )
+                for x in (1 + step * PLANES + place for place in range(PLANES))
+            ])
+            return carry
+
+        lax.fori_loop(0, (nx - 2) // PLANES, inner, 0)
         wait_received(1, slot)
 
-        def inner(x, packs):
-            vector = advance(
-                x, k, slot, lambda f: search[slot, f, x - 1], lambda f: search[slot, f, x + 1]
-            )
-            return packs if last else publish(x, vector, later, packs)
-
-        packs = lax.fori_loop(1, nx - 1, inner, (blank, blank))
+        def settle(planes, packs):
+            vectors = [finish(x, k, slot) for x in planes]
+            for x, vector in zip(planes, vectors):
+                for f in range(fields):
+                    basis[k + 1, f, x] = vector[f]
+            return packs if last else publish(planes, vectors, later, packs)
+
+        packs = lax.fori_loop(
+            0, (nx - 2) // PLANES,
+            lambda step, packs: settle(
+                [1 + step * PLANES + place for place in range(PLANES)], packs
+            ),
+            (blank, blank),
+        )
         wait_received(0, slot)
-        bottom = advance(0, k, slot, lambda f: xin[slot, 0, f], lambda f: search[slot, f, 1])
+        spatial(k, slot, [
+            (0, lambda f: xin[slot, 0, f], lambda f: search[slot, f, 1]),
+            (nx - 1, lambda f: search[slot, f, nx - 2], lambda f: xin[slot, 1, f]),
+        ])
+        packs = settle([0, nx - 1], packs)
         if not last:
-            packs = publish(0, bottom, later, packs)
-        top = advance(
-            nx - 1, k, slot, lambda f: search[slot, f, nx - 2], lambda f: xin[slot, 1, f]
-        )
-        if not last:
-            packs = publish(nx - 1, top, later, packs)
             zout[later, 0], zout[later, 1] = packs
             for axis in range(3):
                 start(axis, later)
@@ -342,7 +380,7 @@
     fields = 2 * levels
     total = sizes[0] * sizes[1] * sizes[2]
     pairs = pair_index(ITERS, ITERS) + 1
-    assert fields * nx <= nz and pairs <= nz
+    assert fields * nx <= nz and pairs <= nz and nx % PLANES == 0
     f32 = jnp.float32
     hbm = pl.BlockSpec(memory_space=pl.ANY)
     vmem = pl.BlockSpec(memory_space=pltpu.VMEM)

time: 75.5 us -> 54.1 us (0.72)
  Pallas kernels: 71.7 us -> 50.2 us
    pallas_call x1, Pallas kernels: 71.7 us -> 50.2 us  [fused(): pl.pallas_call(functools.partial(kernel, levels, sizes), out_shape=(jax.S...]
where the time goes in v2:
time: 54.1 us; the launch traced here: 53.9 us
  Pallas kernels  50.2 us (93%)
  local copies, waits for them, and re-layouts  2.78 us (5%)
  between operations  0.67 us (1%)
    pallas_call x1, Pallas kernels, fused(): pl.pallas_call(functools.partial(kernel, levels, sizes), out_shape=(jax.S...  50.2 us
    unnamed x1, local copies, waits for them, and re-layouts  2.27 us

profile of v2, /device:TPU:0, one launch (start us, length us, event | category | flops | bytes accessed | tf_op | source)
XLA Modules:
  0.0 53.9 jit_solution(5221268720466952364)
XLA Ops:
  0.0 50.2 %krylov.1 = (f32[8,16,16,128]{3,2,1,0:T(8,128)}, f32[8,128]{1,0:T(8,128)S(1)}) custom-call(f32[8,16,16,128]{3,2,1,0:T(8,128)} %bitcast.256, f32[4,16,16,128]{3,2,1,0:T(8,128)} %reaction.1, f32[4,16,16,128]{3,2,1,0:T(8,128)} %transport.1, f32[4,16,16,128]{3,2,1,0:T(8,128)} %congestion.1), custom_call_target="tpu_custom_call" | custom-call | tf_op jit(solution)/shard_map/krylov/pallas_call | solution.py:387
  50.2 0.5 slice.663
  51.4 0.2 conditional.1
  51.6 2.3 %copy.48 = f32[2,4,16,16,128]{4,3,2,1,0:T(8,128)} copy(f32[2,4,16,16,128]{4,3,2,1,0:T(8,128)} %get-tuple-element.260) | data formatting | bytes 2097152
